TPU v7x, 256 devices: a whole 4x4x8 slice. The times are simulated.
256 devices in a mesh: act: 64 (over x, z, core), rep: 4 (over y).
Axes of the slice: x: 4, y: 4, z: 8, core: 2. Of those that a mesh axis runs over, the one named last changes fastest.
Arguments:
- estimated_returns: float32 [512, 131072], P('act', 'rep'), may hold values from -1000 to 1000
- chosen_move_ids: int32 [512, 131072], P('act', 'rep'), may hold values from 0 to 17
- previous_eta: float32 [1], replicated, may hold values from 0.3 to 3
- trust_region_epsilon: float32 [1], replicated, may hold values from 0.02 to 1
Outputs:
- sample_importance: float32 [512, 131072], P('act', 'rep')
- goal_distribution: float32 [18, 131072], P(None, ('rep', 'act'))
- new_temperature: float32 [1], replicated
All inputs are finite; a program needn't handle non-finite values.
Results may differ from a plain program's by a relative error of at most 0.0003.
Values sent between devices are 32-bit elements; how exact they have to be, the bound alone decides.
No kernel may reach another device: no remote copies, remote signals or barrier semaphores. Data moves between devices by JAX's collectives and lax.ppermute only.
A program may use at most 64 MiB of HBM per device.

v0:
```python
import jax
import jax.numpy as jnp
from jax import lax
from jax.sharding import Mesh
from jax.sharding import PartitionSpec as P

NACT = 18
ITERS = 3
ACT = ("act_0", "act_1", "act_2")
REP_ACT = ("rep", "act_0", "act_1", "act_2")


def cut_along(shard, dim, peers):
    shape = shard.shape
    blocks = shard.reshape(*shape[:dim], peers, shape[dim] // peers, *shape[dim + 1 :])
    return jnp.moveaxis(blocks, dim, 0)


def sum_at_owner(shard, axis, dim):
    blocks = cut_along(shard, dim, lax.axis_size(axis))
    arrived = lax.all_to_all(blocks, axis, split_axis=0, concat_axis=0, tiled=True)
    return arrived.sum(axis=0)


def sum_in_two_steps(shard, axes, dim):
    far, near = axes
    own = sum_at_owner(cut_along(shard, dim, lax.axis_size(far)), near, dim + 1)
    return jnp.sum(lax.all_to_all(own, far, 0, 0, tiled=True), axis=0)


def copy_for_each(shard, axis):
    copies = jnp.broadcast_to(shard, (lax.axis_size(axis), *shard.shape))
    return lax.all_to_all(copies, axis, split_axis=0, concat_axis=0, tiled=True)


def over_copies(shard, axis):
    everything = copy_for_each(shard, axis)
    return jnp.sum(everything, axis=0)


def by_axis(shard, axes):
    far, near = axes
    return over_copies(over_copies(shard, near), far)


def together(arrays, axis):
    ends = [0]
    for a in arrays:
        ends.append(ends[-1] + a.size)
    total = by_axis(jnp.concatenate([a.ravel() for a in arrays]), axis)
    return tuple((total[b:e].reshape(a.shape) for a, b, e in zip(arrays, ends, ends[1:])))


def summary_figures(centered_returns, lagrange_eta):
    exponential_term = jnp.exp(centered_returns / lagrange_eta)
    partition_total = jnp.sum(exponential_term, axis=0)
    leading_part = jnp.sum(exponential_term * centered_returns, axis=0)
    trailing_part = jnp.sum(exponential_term * centered_returns * centered_returns, axis=0)
    return (exponential_term, partition_total, leading_part, trailing_part)


def within_situation(partition_total, leading_part, trailing_part, lagrange_eta, move_draws):
    entropy_gap = (
        leading_part / (partition_total * lagrange_eta)
        - jnp.log(partition_total)
        + jnp.log(jnp.float32(move_draws))
    )
    mean_first = leading_part / partition_total
    spread = trailing_part / partition_total - mean_first * mean_first
    return (jnp.sum(entropy_gap), jnp.sum(spread))


def gradient_step(lagrange_eta, ceiling_term, aggregate_relative_entropy, aggregate_deviation):
    change_amount = (
        (ceiling_term - aggregate_relative_entropy)
        * lagrange_eta
        / (1.0 + aggregate_deviation / lagrange_eta)
    )
    return lagrange_eta * jnp.exp(-jnp.tanh(change_amount))


def per_action(probs, ids_block):
    return jnp.stack([jnp.sum(jnp.where(ids_block == k, probs, 0.0), axis=0) for k in range(NACT)])


def scatter_target(probs, ids_block):
    return sum_in_two_steps(per_action(probs, ids_block), (("act_0", "act_1"), "act_2"), 1)


def on_device(estimated_returns, chosen_move_ids, previous_eta, trust_region_epsilon):
    lagrange_eta = previous_eta[0]
    ceiling_term = trust_region_epsilon[0]
    move_draws = estimated_returns.shape[0] * lax.axis_size(ACT)
    q_rows = lax.all_to_all(estimated_returns, ACT, split_axis=1, concat_axis=0, tiled=True)
    tally_number = q_rows.shape[1] * lax.axis_size(ACT) * lax.axis_size("rep")
    centered_returns = q_rows - jnp.max(q_rows, axis=0, keepdims=True)
    for step in range(ITERS):
        exponential_term, partition_total, leading_part, trailing_part = summary_figures(
            centered_returns, lagrange_eta
        )
        shard_divergence, shard_value_spread = within_situation(
            partition_total, leading_part, trailing_part, lagrange_eta, move_draws
        )
        aggregate_relative_entropy, aggregate_deviation = together(
            (shard_divergence, shard_value_spread), (("act_0", "act_1"), ("act_2", "rep"))
        )
        lagrange_eta = gradient_step(
            lagrange_eta,
            ceiling_term,
            aggregate_relative_entropy / tally_number,
            aggregate_deviation / tally_number,
        )
    exponential_term, partition_total, leading_part, trailing_part = summary_figures(
        centered_returns, lagrange_eta
    )
    probs_rows = exponential_term / partition_total
    sample_importance = lax.all_to_all(
        move_draws * probs_rows, ACT, split_axis=0, concat_axis=1, tiled=True
    )
    goal_distribution = scatter_target(sample_importance / jnp.float32(move_draws), chosen_move_ids)
    return (sample_importance, goal_distribution, jnp.reshape(lagrange_eta, (1,)))


def solution(mesh):
    split = Mesh(
        mesh.devices.reshape(4, 8, 2, mesh.shape["rep"]), ("act_0", "act_1", "act_2", "rep")
    )
    placed = (P(ACT, "rep"), P(ACT, "rep"), P(), P())
    return jax.shard_map(
        on_device,
        mesh=split,
        in_specs=placed,
        out_specs=(P(ACT, "rep"), P(None, REP_ACT), P()),
        check_vma=False,
    )
```

profile of v0, /device:TPU:32, one launch (start us, length us, event | category | flops | bytes accessed | tf_op | source)
XLA Modules:
  0.0 227.9 jit_solution(15470701140509389967)
XLA Ops:
  0.6 11.6 %all-to-all-start = ((f32[8,64,512]{2,0,1:T(8,128)}), f32[8,64,512]{2,0,1:T(8,128)S(1)}, u32[]{:S(2)}, u32[]{:S(2)}) async-start(f32[8,64,512]{2,0,1:T(8,128)} %bitcast.90), calls=%async_computation | async-start | bytes 2097152 | tf_op jit(solution)/shard_map/all_to_all | solution.py:94
  12.9 27.2 %all-to-all-done = f32[8,64,512]{2,0,1:T(8,128)S(1)} async-done(((f32[8,64,512]{2,0,1:T(8,128)}), f32[8,64,512]{2,0,1:T(8,128)S(1)}, u32[]{:S(2)}, u32[]{:S(2)}) %all-to-all-start) | async-done | bytes 1048608 | tf_op jit(solution)/shard_map/all_to_all | solution.py:94
  40.5 0.6 add_reduce_fusion.2
  41.2 1.4 pad_maximum_fusion
  42.5 9.5 %all_to_all.75 = f32[8,1,2]{2,1,0:T(1,128)S(1)} all-to-all(f32[8,1,2]{2,1,0:T(1,128)S(1)} %broadcast_in_dim.41), channel_id=1, replica_groups=mesh['act_0'=4,'act_1'=8,'act_2'=2,'rep'=4] {'act_2','rep'}, dimensions={0} | all-to-all | bytes 128 | tf_op jit(solution)/shard_map/all_to_all | solution.py:33
  52.1 0.6 broadcast_in_dim.42
  52.7 6.5 %all-to-all-start.2 = ((f32[32,1,2]{2,1,0:T(1,128)}), f32[32,1,2]{2,1,0:T(1,128)S(1)}, u32[]{:S(2)}, u32[]{:S(2)}) async-start(f32[32,1,2]{2,1,0:T(1,128)} %broadcast_in_dim.42), calls=%async_computation.2 | async-start | bytes 32768 | tf_op jit(solution)/shard_map/all_to_all | solution.py:33
  59.8 7.9 %all-to-all-done.2 = f32[32,1,2]{2,1,0:T(1,128)S(1)} async-done(((f32[32,1,2]{2,1,0:T(1,128)}), f32[32,1,2]{2,1,0:T(1,128)S(1)}, u32[]{:S(2)}, u32[]{:S(2)}) %all-to-all-start.2) | async-done | bytes 288 | tf_op jit(solution)/shard_map/all_to_all | solution.py:33
  70.8 1.4 pad_maximum_fusion.1
  72.2 7.6 %all_to_all.76 = f32[8,1,2]{2,1,0:T(1,128)S(1)} all-to-all(f32[8,1,2]{2,1,0:T(1,128)S(1)} %broadcast_in_dim.43), channel_id=1, replica_groups=mesh['act_0'=4,'act_1'=8,'act_2'=2,'rep'=4] {'act_2','rep'}, dimensions={0} | all-to-all | bytes 128 | tf_op jit(solution)/shard_map/all_to_all | solution.py:33
  79.8 12.8 %all_to_all.77 = f32[32,1,2]{2,1,0:T(1,128)S(1)} all-to-all(f32[32,1,2]{2,1,0:T(1,128)S(1)} %broadcast_in_dim.44), channel_id=1, replica_groups=mesh['act_0'=4,'act_1'=8,'act_2'=2,'rep'=4] {'act_0','act_1'}, dimensions={0} | all-to-all | bytes 512 | tf_op jit(solution)/shard_map/all_to_all | solution.py:33
  95.7 1.4 pad_maximum_fusion.2
  97.1 7.6 %all_to_all.78 = f32[8,1,2]{2,1,0:T(1,128)S(1)} all-to-all(f32[8,1,2]{2,1,0:T(1,128)S(1)} %broadcast_in_dim.45), channel_id=1, replica_groups=mesh['act_0'=4,'act_1'=8,'act_2'=2,'rep'=4] {'act_2','rep'}, dimensions={0} | all-to-all | bytes 128 | tf_op jit(solution)/shard_map/all_to_all | solution.py:33
  104.7 12.8 %all_to_all.79 = f32[32,1,2]{2,1,0:T(1,128)S(1)} all-to-all(f32[32,1,2]{2,1,0:T(1,128)S(1)} %broadcast_in_dim.46), channel_id=1, replica_groups=mesh['act_0'=4,'act_1'=8,'act_2'=2,'rep'=4] {'act_0','act_1'}, dimensions={0} | all-to-all | bytes 512 | tf_op jit(solution)/shard_map/all_to_all | solution.py:33
  120.0 32.8 %all_to_all.80 = f32[64,8,512]{2,1,0:T(8,128)S(1)} all-to-all(f32[64,8,512]{2,1,0:T(8,128)S(1)} %divide_multiply_fusion), channel_id=1, replica_groups=mesh['act_0'=4,'act_1'=8,'act_2'=2,'rep'=4] {'act_0','act_1','act_2'}, dimensions={0} | all-to-all | bytes 2097152 | tf_op jit(solution)/shard_map/all_to_all | solution.py:117
  152.8 10.5 %select_reduce_fusion = (f32[32768]{0:T(1024)S(1)}, f32[32768]{0:T(1024)S(1)}, f32[32768]{0:T(1024)S(1)}, f32[32768]{0:T(1024)S(1)}, f32[32768]{0:T(1024)S(1)}, ...) fusion(s32[8,32768]{1,0:T(8,128)S(1)} %copy-done.1, ...), kind=kLoop, calls=%fused_computation.17 | loop fusion | flops 13828096 | bytes 4456448 | tf_op jit(solution)/shard_map/reduce_sum | solution.py:83
  164.2 1.4 copy-done
  165.7 3.3 %reshape.176 = f32[32,18,2,512]{3,2,0,1:T(2,128)S(1)} reshape(f32[32,18,1024]{2,0,1:T(8,128)} %bitcast.89) | data formatting | bytes 4718592 | tf_op jit(solution)/shard_map/reshape | solution.py:15
  169.5 5.6 %all_to_all.81 = f32[2,32,18,512]{3,1,2,0:T(8,128)S(1)} all-to-all(f32[2,32,18,512]{3,1,2,0:T(8,128)S(1)} %copy.19), channel_id=1, replica_groups=mesh['act_0'=4,'act_1'=8,'act_2'=2,'rep'=4] {'act_2'}, dimensions={0} | all-to-all | bytes 4718592 | tf_op jit(solution)/shard_map/all_to_all | solution.py:21
  175.1 1.3 reduce_sum.418
  176.4 2.0 copy.20
  178.4 46.7 %all_to_all.82 = f32[32,18,512]{2,1,0:T(8,128)S(1)} all-to-all(f32[32,18,512]{2,1,0:T(8,128)S(1)} %copy.20), channel_id=1, replica_groups=mesh['act_0'=4,'act_1'=8,'act_2'=2,'rep'=4] {'act_0','act_1'}, dimensions={0} | all-to-all | bytes 2359296 | tf_op jit(solution)/shard_map/all_to_all | solution.py:28
  225.1 0.7 reduce_sum.419
  225.8 1.0 copy.53
  (62 shorter events, 6.0 us)
Async XLA Ops:
  0.6 39.5 %all-to-all-start = ((f32[8,64,512]{2,0,1:T(8,128)}), f32[8,64,512]{2,0,1:T(8,128)S(1)}, u32[]{:S(2)}, u32[]{:S(2)}) async-start(f32[8,64,512]{2,0,1:T(8,128)} %bitcast.90), calls=%async_computation | async-start | bytes 2097152 | tf_op jit(solution)/shard_map/all_to_all | solution.py:94
  52.7 15.0 %all-to-all-start.2 = ((f32[32,1,2]{2,1,0:T(1,128)}), f32[32,1,2]{2,1,0:T(1,128)S(1)}, u32[]{:S(2)}, u32[]{:S(2)}) async-start(f32[32,1,2]{2,1,0:T(1,128)} %broadcast_in_dim.42), calls=%async_computation.2 | async-start | bytes 32768 | tf_op jit(solution)/shard_map/all_to_all | solution.py:33
  119.8 33.0 %copy-start.1 = (s32[8,32768]{1,0:T(8,128)S(1)}, s32[8,32768]{1,0:T(8,128)}, u32[]{:S(2)}) copy-start(s32[8,32768]{1,0:T(8,128)} %param.5) | copy-start | bytes 3145732
  164.2 1.4 copy-start
where the time goes:
time: 229 us; the launch traced here: 228 us
  blocking collectives  135 us (59%)
  waiting for transfers between devices  35.1 us (15%)
  other arithmetic  20.2 us (9%)
  starting transfers between devices  18.1 us (8%)
  local copies, waits for them, and re-layouts  11.3 us (5%)
  between operations  7.81 us (3%)
    all_to_all x5, blocking collectives, copy_for_each(): return lax.all_to_all(copies, axis, split_axis=0, concat_axis=0, tiled=True)  50.3 us
    all_to_all x1, blocking collectives, sum_in_two_steps(): return jnp.sum(lax.all_to_all(own, far, 0, 0, tiled=True), axis=0)  46.7 us
    all_to_all x1, blocking collectives, on_device(): lax.all_to_all(move_draws * probs_rows, ACT, split_axis=0, concat_axis=1,...  32.8 us
    all_to_all x1, waiting for transfers between devices, on_device(): lax.all_to_all(estimated_returns, ACT, split_axis=1, concat_axis=0, tiled...  27.2 us
    all_to_all x1, starting transfers between devices, on_device(): lax.all_to_all(estimated_returns, ACT, split_axis=1, concat_axis=0, tiled...  11.6 us
    reduce_sum x1, other arithmetic, per_action(): jnp.sum(jnp.where(ids_block == k, probs, 0.0), axis=0)  10.5 us
    all_to_all x1, waiting for transfers between devices, copy_for_each(): return lax.all_to_all(copies, axis, split_axis=0, concat_axis=0, tiled=True)  7.92 us
    all_to_all x1, starting transfers between devices, copy_for_each(): return lax.all_to_all(copies, axis, split_axis=0, concat_axis=0, tiled=True)  6.46 us
  transfers between devices with their start and end apart: 2, of which 2 were waited for; matrix products, arithmetic and copies ran while one was open for 0% of the time, Pallas kernels for 0%

commit v1 on v0

--- a/solution.py
+++ b/solution.py
@@ -114,8 +114,11 @@
         centered_returns, lagrange_eta
     )
     probs_rows = exponential_term / partition_total
-    sample_importance = lax.all_to_all(
-        move_draws * probs_rows, ACT, split_axis=0, concat_axis=1, tiled=True
+    sample_importance = jnp.concatenate(
+        lax.all_to_all(
+            jnp.stack(jnp.split(move_draws * probs_rows, lax.axis_size(ACT), axis=0)), ACT, 0, 0
+        ),
+        axis=1,
     )
     goal_distribution = scatter_target(sample_importance / jnp.float32(move_draws), chosen_move_ids)
     return (sample_importance, goal_distribution, jnp.reshape(lagrange_eta, (1,)))

time: 229 us -> 229 us (level)
  no operation moved by 1% of the time
where the time goes in v1:
time: 229 us
  blocking collectives  135 us (59%)
  waiting for transfers between devices  35.1 us (15%)
  other arithmetic  20.2 us (9%)
  starting transfers between devices  18.1 us (8%)
  local copies, waits for them, and re-layouts  11.5 us (5%)
  between operations  8.32 us (4%)
    all_to_all x5, blocking collectives, copy_for_each(): return lax.all_to_all(copies, axis, split_axis=0, concat_axis=0, tiled=True)  50.3 us
    all_to_all x1, blocking collectives, sum_in_two_steps(): return jnp.sum(lax.all_to_all(own, far, 0, 0, tiled=True), axis=0)  46.7 us
    all_to_all x1, blocking collectives, on_device(): lax.all_to_all(jnp.stack(jnp.split(move_draws * probs_rows, lax.axis_size...  32.6 us
    all_to_all x1, waiting for transfers between devices, on_device(): lax.all_to_all(estimated_returns, ACT, split_axis=1, concat_axis=0, tiled...  27.2 us
    all_to_all x1, starting transfers between devices, on_device(): lax.all_to_all(estimated_returns, ACT, split_axis=1, concat_axis=0, tiled...  11.6 us
    reduce_sum x1, other arithmetic, per_action(): jnp.sum(jnp.where(ids_block == k, probs, 0.0), axis=0)  10.5 us
    all_to_all x1, waiting for transfers between devices, copy_for_each(): return lax.all_to_all(copies, axis, split_axis=0, concat_axis=0, tiled=True)  7.92 us
    all_to_all x1, starting transfers between devices, copy_for_each(): return lax.all_to_all(copies, axis, split_axis=0, concat_axis=0, tiled=True)  6.46 us
  transfers between devices with their start and end apart: 2, of which 2 were waited for; matrix products, arithmetic and copies ran while one was open for 0% of the time, Pallas kernels for 0%

profile of v1, /device:TPU:32, one launch (start us, length us, event | category | flops | bytes accessed | tf_op | source)
XLA Modules:
  0.0 228.5 jit_solution(10513821680011588671)
XLA Ops:
  0.6 11.6 %all-to-all-start = ((f32[8,64,512]{2,0,1:T(8,128)}), f32[8,64,512]{2,0,1:T(8,128)S(1)}, u32[]{:S(2)}, u32[]{:S(2)}) async-start(f32[8,64,512]{2,0,1:T(8,128)} %bitcast.320), calls=%async_computation | async-start | bytes 2097152 | tf_op jit(solution)/shard_map/all_to_all | solution.py:94
  12.9 27.2 %all-to-all-done = f32[8,64,512]{2,0,1:T(8,128)S(1)} async-done(((f32[8,64,512]{2,0,1:T(8,128)}), f32[8,64,512]{2,0,1:T(8,128)S(1)}, u32[]{:S(2)}, u32[]{:S(2)}) %all-to-all-start) | async-done | bytes 1048608 | tf_op jit(solution)/shard_map/all_to_all | solution.py:94
  40.5 0.6 add_reduce_fusion.2
  41.2 1.4 pad_maximum_fusion
  42.5 9.5 %all_to_all.70 = f32[8,1,2]{2,1,0:T(1,128)S(1)} all-to-all(f32[8,1,2]{2,1,0:T(1,128)S(1)} %broadcast_in_dim.41), channel_id=1, replica_groups=mesh['act_0'=4,'act_1'=8,'act_2'=2,'rep'=4] {'act_2','rep'}, dimensions={0} | all-to-all | bytes 128 | tf_op jit(solution)/shard_map/all_to_all | solution.py:33
  52.1 0.6 broadcast_in_dim.42
  52.7 6.5 %all-to-all-start.2 = ((f32[32,1,2]{2,1,0:T(1,128)}), f32[32,1,2]{2,1,0:T(1,128)S(1)}, u32[]{:S(2)}, u32[]{:S(2)}) async-start(f32[32,1,2]{2,1,0:T(1,128)} %broadcast_in_dim.42), calls=%async_computation.2 | async-start | bytes 32768 | tf_op jit(solution)/shard_map/all_to_all | solution.py:33
  59.8 7.9 %all-to-all-done.2 = f32[32,1,2]{2,1,0:T(1,128)S(1)} async-done(((f32[32,1,2]{2,1,0:T(1,128)}), f32[32,1,2]{2,1,0:T(1,128)S(1)}, u32[]{:S(2)}, u32[]{:S(2)}) %all-to-all-start.2) | async-done | bytes 288 | tf_op jit(solution)/shard_map/all_to_all | solution.py:33
  70.8 1.4 pad_maximum_fusion.1
  72.2 7.6 %all_to_all.71 = f32[8,1,2]{2,1,0:T(1,128)S(1)} all-to-all(f32[8,1,2]{2,1,0:T(1,128)S(1)} %broadcast_in_dim.43), channel_id=1, replica_groups=mesh['act_0'=4,'act_1'=8,'act_2'=2,'rep'=4] {'act_2','rep'}, dimensions={0} | all-to-all | bytes 128 | tf_op jit(solution)/shard_map/all_to_all | solution.py:33
  79.8 12.8 %all_to_all.72 = f32[32,1,2]{2,1,0:T(1,128)S(1)} all-to-all(f32[32,1,2]{2,1,0:T(1,128)S(1)} %broadcast_in_dim.44), channel_id=1, replica_groups=mesh['act_0'=4,'act_1'=8,'act_2'=2,'rep'=4] {'act_0','act_1'}, dimensions={0} | all-to-all | bytes 512 | tf_op jit(solution)/shard_map/all_to_all | solution.py:33
  95.7 1.4 pad_maximum_fusion.2
  97.1 7.6 %all_to_all.73 = f32[8,1,2]{2,1,0:T(1,128)S(1)} all-to-all(f32[8,1,2]{2,1,0:T(1,128)S(1)} %broadcast_in_dim.45), channel_id=1, replica_groups=mesh['act_0'=4,'act_1'=8,'act_2'=2,'rep'=4] {'act_2','rep'}, dimensions={0} | all-to-all | bytes 128 | tf_op jit(solution)/shard_map/all_to_all | solution.py:33
  104.7 12.8 %all_to_all.74 = f32[32,1,2]{2,1,0:T(1,128)S(1)} all-to-all(f32[32,1,2]{2,1,0:T(1,128)S(1)} %broadcast_in_dim.46), channel_id=1, replica_groups=mesh['act_0'=4,'act_1'=8,'act_2'=2,'rep'=4] {'act_0','act_1'}, dimensions={0} | all-to-all | bytes 512 | tf_op jit(solution)/shard_map/all_to_all | solution.py:33
  120.8 32.6 %all_to_all.75 = f32[64,8,512]{2,1,0:T(8,128)S(1)} all-to-all(f32[64,8,512]{2,1,0:T(8,128)S(1)} %constant_dynamic-update-slice_fusion), channel_id=1, replica_groups=mesh['act_0'=4,'act_1'=8,'act_2'=2,'rep'=4] {'act_0','act_1','act_2'}, dimensions={0} | all-to-all | bytes 2097152 | tf_op jit(solution)/shard_map/all_to_all | solution.py:118
  153.4 10.5 %select_reduce_fusion = (f32[32768]{0:T(1024)S(1)}, f32[32768]{0:T(1024)S(1)}, f32[32768]{0:T(1024)S(1)}, f32[32768]{0:T(1024)S(1)}, f32[32768]{0:T(1024)S(1)}, ...) fusion(s32[8,32768]{1,0:T(8,128)S(1)} %copy-done.1, ...), kind=kLoop, calls=%fused_computation.6 | loop fusion | flops 13828096 | bytes 4456448 | tf_op jit(solution)/shard_map/reduce_sum | solution.py:83
  164.9 1.4 copy-done
  166.3 3.3 %reshape.171 = f32[32,18,2,512]{3,2,0,1:T(2,128)S(1)} reshape(f32[32,18,1024]{2,0,1:T(8,128)} %bitcast.319) | data formatting | bytes 4718592 | tf_op jit(solution)/shard_map/reshape | solution.py:15
  170.1 5.6 %all_to_all.76 = f32[2,32,18,512]{3,1,2,0:T(8,128)S(1)} all-to-all(f32[2,32,18,512]{3,1,2,0:T(8,128)S(1)} %copy.19), channel_id=1, replica_groups=mesh['act_0'=4,'act_1'=8,'act_2'=2,'rep'=4] {'act_2'}, dimensions={0} | all-to-all | bytes 4718592 | tf_op jit(solution)/shard_map/all_to_all | solution.py:21
  175.7 1.3 reduce_sum.418
  177.0 2.0 copy.20
  179.0 46.7 %all_to_all.77 = f32[32,18,512]{2,1,0:T(8,128)S(1)} all-to-all(f32[32,18,512]{2,1,0:T(8,128)S(1)} %copy.20), channel_id=1, replica_groups=mesh['act_0'=4,'act_1'=8,'act_2'=2,'rep'=4] {'act_0','act_1'}, dimensions={0} | all-to-all | bytes 2359296 | tf_op jit(solution)/shard_map/all_to_all | solution.py:28
  225.7 0.7 reduce_sum.419
  226.4 1.0 copy.116
  (126 shorter events, 6.2 us)
Async XLA Ops:
  0.6 39.5 %all-to-all-start = ((f32[8,64,512]{2,0,1:T(8,128)}), f32[8,64,512]{2,0,1:T(8,128)S(1)}, u32[]{:S(2)}, u32[]{:S(2)}) async-start(f32[8,64,512]{2,0,1:T(8,128)} %bitcast.320), calls=%async_computation | async-start | bytes 2097152 | tf_op jit(solution)/shard_map/all_to_all | solution.py:94
  52.7 15.0 %all-to-all-start.2 = ((f32[32,1,2]{2,1,0:T(1,128)}), f32[32,1,2]{2,1,0:T(1,128)S(1)}, u32[]{:S(2)}, u32[]{:S(2)}) async-start(f32[32,1,2]{2,1,0:T(1,128)} %broadcast_in_dim.42), calls=%async_computation.2 | async-start | bytes 32768 | tf_op jit(solution)/shard_map/all_to_all | solution.py:33
  120.0 33.4 %copy-start.1 = (s32[8,32768]{1,0:T(8,128)S(1)}, s32[8,32768]{1,0:T(8,128)}, u32[]{:S(2)}) copy-start(s32[8,32768]{1,0:T(8,128)} %param.5) | copy-start | bytes 3145732
  164.8 1.4 copy-start
